TPU v7x, 128 devices: a whole 4x4x4 slice. The times are simulated.
128 devices in a mesh: dp: 8 (over x, core), expert: 16 (over y, z).
Axes of the slice: x: 4, y: 4, z: 4, core: 2. Of those that a mesh axis runs over, the one named last changes fastest.
Arguments:
- grads: bfloat16 [131072, 4096], P(('dp', 'expert')), may hold values from -6 to 6
- block_expert: int32 [1024, 1], P(('dp', 'expert')), may hold values from 0 to 15; in each aligned block of 8 rows (0 to 7, 8 to 15, ...) at most 2 rows name the same one
- sketch: bfloat16 [16, 256, 4096], P('expert', None, 'dp'), may hold values from -0.09375 to 0.09375
Outputs:
- factor: bfloat16 [16, 256, 4096], P('expert')
Inputs may be any that keep to these rules, and one draw needn't show every extreme that they name: `block_expert`: among the 8 blocks of one device, at most 2 belong to one expert, and every expert has some block.
All inputs are finite; a program needn't handle non-finite values.
Results may differ from a plain program's by a relative error of at most 0.0031.
Values may be sent and summed in bfloat16 or wider, within the bound.
A program may use at most 256 MiB of HBM per device.

v0:
```python
import jax
import jax.numpy as jnp
from jax import lax
from jax.sharding import PartitionSpec as P

D = 4096
BLOCK = 128
CAP = 2
ITERS = 5
EPSILON = 1e-06


def in_blocks(x, dim, length):
    lengths = x.shape
    parts = x.reshape(*lengths[:dim], length, lengths[dim] // length, *lengths[dim + 1 :])
    return jnp.moveaxis(parts, dim, 0)


def cut_rows(length, count):
    turn = length // count
    if turn >= 8:
        turn -= turn % 8
    return [turn * k for k in range(1, count)]


def laid_out(parts, dim):
    parts = jnp.moveaxis(parts, 0, dim)
    lengths = parts.shape
    return parts.reshape(*lengths[:dim], lengths[dim] * lengths[dim + 1], *lengths[dim + 2 :])


def cut_exchange(x, axis, pieces, split_dim, concat_dim):
    parts = in_blocks(x, split_dim, lax.axis_size(axis))
    split_at = max(range(1, max(2, parts.ndim - 1)), key=lambda d: parts.shape[d])
    gathered = []
    for piece in jnp.split(parts, cut_rows(parts.shape[split_at], pieces), axis=split_at):
        if piece.size:
            gathered.append(lax.all_to_all(piece, axis, split_axis=0, concat_axis=0, tiled=True))
    return laid_out(jnp.concatenate(gathered, axis=split_at), concat_dim)


def newton_step(iterate, inner):
    return 1.5 * iterate - 0.5 * jnp.dot(inner, iterate, precision=lax.Precision.HIGHEST)


def shards(grads, block_expert, sketch):
    count_blocks = block_expert.shape[0]
    columns = grads.shape[1]
    experts = lax.axis_size("expert")
    replicas = lax.axis_size("dp")
    blocks = grads.reshape(count_blocks, BLOCK, columns)
    owners = block_expert[:, 0]
    same_owner = owners[None, :] == owners[:, None]
    earlier = lax.broadcasted_iota(
        jnp.int32, (count_blocks, count_blocks), 1
    ) < lax.broadcasted_iota(jnp.int32, (count_blocks, count_blocks), 0)
    places = jnp.sum((same_owner & earlier).astype(jnp.int32), axis=1)
    targets = owners * CAP + places
    outgoing = jnp.zeros((experts * CAP, BLOCK, columns), jnp.bfloat16).at[targets].set(blocks)
    outgoing = outgoing.reshape(experts, CAP * BLOCK, columns)
    incoming = cut_exchange(outgoing, "expert", 2, 0, 0)
    arrived = incoming.reshape(experts * CAP * BLOCK, columns)
    basis_full = lax.all_gather(sketch, "dp", axis=2, tiled=True)[0]
    projected = lax.dot_general(
        basis_full, arrived, (((1,), (1,)), ((), ())), preferred_element_type=jnp.float32
    ).astype(jnp.bfloat16)
    partial_term = jnp.dot(projected, arrived, preferred_element_type=jnp.float32)
    basis_gram = lax.dot_general(
        basis_full, basis_full, (((1,), (1,)), ((), ())), preferred_element_type=jnp.float32
    )
    average = float(BLOCK * count_blocks * replicas)
    gradient_term = lax.psum(partial_term, "dp")
    unscaled = (
        jnp.dot(basis_gram, basis_full.astype(jnp.float32), precision=lax.Precision.HIGHEST)
        + gradient_term / average
    )
    iterate = unscaled / jnp.sqrt(jnp.sum(unscaled * unscaled) + EPSILON)
    for step in range(ITERS):
        inner = lax.dot_general(
            iterate, iterate, (((1,), (1,)), ((), ())), precision=lax.Precision.HIGHEST
        )
        iterate = newton_step(iterate, inner)
    return (iterate * D**0.5).astype(jnp.bfloat16)[None]


def solution(mesh):
    in_specs = (P(("dp", "expert"), None), P(("dp", "expert"), None), P("expert", None, "dp"))
    out_specs = P("expert", None, None)
    return jax.shard_map(shards, mesh=mesh, in_specs=in_specs, out_specs=out_specs, check_vma=False)
```

profile of v0, /device:TPU:0, one launch (start us, length us, event | category | flops | bytes accessed | tf_op | source)
XLA Modules:
  0.0 766.7 jit_solution(16272449002042471784)
XLA Ops:
  6.5 0.9 convert_reduce_fusion
  7.4 0.7 fusion.16
  8.1 11.0 %broadcast_in_dim.7 = bf16[32,128,4096]{2,1,0:T(8,128)(2,1)} broadcast(bf16[]{:T(256)} %constant.10.clone.1), dimensions={} | broadcast | bytes 33554432 | tf_op jit(solution)/shard_map/broadcast_in_dim | solution.py:59
  19.1 21.4 %scatter_fusion = bf16[32,128,4096]{2,1,0:T(8,128)(2,1)} fusion(bf16[32,128,4096]{2,1,0:T(8,128)(2,1)} %broadcast_in_dim.7, s32[8]{0:T(128)S(1)} %fusion.16, bf16[8,128,4096]{2,1,0:T(8,128)(2,1)} %bitcast.44), kind=kCustom, calls=%fused_computation | custom fusion | bytes 25165856 | tf_op jit(solution)/shard_map/scatter | solution.py:59
  40.5 18.2 %fusion.17 = (bf16[16,1,128,4096]{3,2,1,0:T(8,128)(2,1)S(1)}, bf16[16,1,128,4096]{3,2,1,0:T(8,128)(2,1)}) fusion(bf16[16,1,256,4096]{3,2,1,0:T(8,128)(2,1)} %bitcast.42), kind=kLoop, calls=%fused_computation.31 | loop fusion | bytes 67108864 | tf_op jit(solution)/shard_map/split | solution.py:36
  58.7 195.6 %all_to_all.10 = bf16[16,1,128,4096]{3,2,1,0:T(8,128)(2,1)} all-to-all(bf16[16,1,128,4096]{3,2,1,0:T(8,128)(2,1)S(1)} %get-tuple-element.5), channel_id=1, replica_groups=mesh['dp'=8,'expert'=16] {'expert'}, dimensions={0} | all-to-all | bytes 33554432 | tf_op jit(solution)/shard_map/all_to_all | solution.py:38
  254.3 5.1 all-to-all-start.1
  259.4 0.0 all-gather.2.cloned.1.call-start
  259.5 0.7 all-gather.2.cloned.1.call-update
  260.1 0.0 all-reduce.2.cloned.1.call-start
  260.2 296.6 %all-to-all-done.1 = bf16[16,1,128,4096]{3,2,1,0:T(8,128)(2,1)} async-done(((bf16[16,1,128,4096]{3,2,1,0:T(8,128)(2,1)}), bf16[16,1,128,4096]{3,2,1,0:T(8,128)(2,1)}, u32[]{:S(2)}, u32[]{:S(2)}) %all-to-all-start.1) | async-done | bytes 16777248 | tf_op jit(solution)/shard_map/all_to_all | solution.py:38
  556.8 22.8 %pad_maximum_fusion = bf16[16,1,256,4096]{3,2,1,0:T(8,128)(2,1)} fusion(bf16[16,1,128,4096]{3,2,1,0:T(8,128)(2,1)} %all-to-all-done.1, bf16[16,1,128,4096]{3,2,1,0:T(8,128)(2,1)} %all_to_all.10), kind=kLoop, calls=%fused_computation.1 | loop fusion | flops 67108864 | bytes 67108864 | tf_op jit(solution)/shard_map/concatenate | solution.py:39
  579.6 0.0 all-gather.2.cloned.1.call-done
  579.6 47.4 %fusion.8 = f32[256,4096]{1,0:T(8,128)} fusion(bf16[4096,4096]{1,0:T(8,128)(2,1)} %bitcast.43, bf16[1,256,4096]{2,1,0:T(8,128)(2,1)} %all-gather.2.cloned.1.call-done), kind=kOutput, calls=%fused_computation.18 | convolution fusion | flops 17180917760 | bytes 39845888 | tf_op jit(solution)/shard_map/dot_general | solution.py:67
  627.0 0.0 copy-start.1
  627.0 0.0 all-reduce.2.cloned.1.call-update
  627.0 1.6 copy-done.1
  628.6 0.7 fusion.12
  629.3 73.8 %all-reduce.2.cloned.1.call-done = f32[256,4096]{1,0:T(8,128)} async-done(((f32[256,4096]{1,0:T(8,128)}), f32[256,4096]{1,0:T(8,128)}) %all-reduce.2.cloned.1.call-update) | async-done | bytes 4194320 | tf_op jit(solution)/shard_map/psum | solution.py:72
  703.1 7.3 multiply_reduce_fusion
  711.1 0.0 copy-start
  711.1 12.2 %fusion.14 = f32[256,256]{1,0:T(8,128)S(1)} fusion(f32[256,4096]{1,0:T(8,128)} %get-tuple-element.8, f32[]{:T(128)S(6)} %sqrt.3), kind=kOutput, calls=%fused_computation.24 | convolution fusion | flops 3222274048 | bytes 4456452 | tf_op jit(solution)/shard_map/dot_general | solution.py:79
  723.3 0.0 copy-done
  723.3 4.1 fusion.4
  727.5 3.5 fusion.18
  731.0 4.1 fusion.3
  735.1 3.9 fusion.19
  739.1 4.1 fusion.2
  743.2 3.5 fusion.20
  746.7 4.3 fusion.1
  751.0 3.5 fusion.21
  754.6 5.1 fusion.7
Async XLA Ops:
  254.3 302.5 %all-to-all-start.1 = ((bf16[16,1,128,4096]{3,2,1,0:T(8,128)(2,1)}), bf16[16,1,128,4096]{3,2,1,0:T(8,128)(2,1)}, u32[]{:S(2)}, u32[]{:S(2)}) async-start(bf16[16,1,128,4096]{3,2,1,0:T(8,128)(2,1)} %get-tuple-element.6), calls=%async_computation.1 | async-start | bytes 33554432 | tf_op jit(solution)/shard_map/all_to_all | solution.py:38
  259.4 320.2 %all-gather.2.cloned.1.call-start = ((), (), s32[]{:S(2)}) async-start(), calls=%async_computation.2 | async-start | bytes 2359296 | tf_op jit(solution)/shard_map/all_gather | solution.py:63
  260.1 443.0 %all-reduce.2.cloned.1.call-start = ((), (), s32[]{:S(2)}) async-start(), calls=%async_computation.3 | async-start | bytes 8388608 | tf_op jit(solution)/shard_map/psum | solution.py:72
  627.0 1.6 copy-start.1
  711.1 12.2 %copy-start = (f32[256,4096]{1,0:T(8,128)S(1)}, f32[256,4096]{1,0:T(8,128)}, u32[]{:S(2)}) copy-start(f32[256,4096]{1,0:T(8,128)} %get-tuple-element.8) | copy-start | bytes 12582916
Sparse Core Ops, SparseCore 0:
  261.9 26.6 all-gather.1
  627.2 75.9 all-reduce.1
where the time goes:
time: 775 us; the launch traced here: 767 us
  waiting for transfers between devices  371 us (48%)
  blocking collectives  196 us (25%)
  matrix products  104 us (13%)
  local copies, waits for them, and re-layouts  52.2 us (7%)
  other arithmetic  24.4 us (3%)
  between operations  14.4 us (2%)
    all_to_all x1, waiting for transfers between devices, cut_exchange(): lax.all_to_all(piece, axis, split_axis=0, concat_axis=0, tiled=True)  297 us
    all_to_all x1, blocking collectives, cut_exchange(): lax.all_to_all(piece, axis, split_axis=0, concat_axis=0, tiled=True)  196 us
    psum x1, waiting for transfers between devices, shards(): gradient_term = lax.psum(partial_term, 'dp')  73.8 us
    dot_general x1, matrix products, shards(): jnp.dot(projected, arrived, preferred_element_type=jnp.float32)  47.4 us
    dot_general x5, matrix products, shards(): lax.dot_general(iterate, iterate, (((1,), (1,)), ((), ())), precision=lax...  26.8 us
    concatenate x1, other arithmetic, cut_exchange(): return laid_out(jnp.concatenate(gathered, axis=split_at), concat_dim)  22.8 us
    dot_general x5, matrix products, newton_step(): jnp.dot(inner, iterate, precision=lax.Precision.HIGHEST)  21.7 us
    scatter x1, local copies, waits for them, and re-layouts, shards(): jnp.zeros((experts * CAP, BLOCK, columns), jnp.bfloat16).at[targets]  21.4 us
  transfers between devices with their start and end apart: 3, of which 2 were waited for; matrix products, arithmetic and copies ran while one was open for 3% of the time, Pallas kernels for 0%

commit v1 on v0

--- a/solution.py
+++ b/solution.py
@@ -69,7 +69,11 @@
         basis_full, basis_full, (((1,), (1,)), ((), ())), preferred_element_type=jnp.float32
     )
     average = float(BLOCK * count_blocks * replicas)
-    gradient_term = lax.psum(partial_term, "dp")
+    gradient_term = partial_term
+    for hop in (1, 2, 4):
+        gradient_term = gradient_term + lax.ppermute(
+            gradient_term, "dp", [(dev, dev ^ hop) for dev in range(8)]
+        )
     unscaled = (
         jnp.dot(basis_gram, basis_full.astype(jnp.float32), precision=lax.Precision.HIGHEST)
         + gradient_term / average

time: 775 us -> 895 us (1.15)
  waiting for transfers between devices: 371 us -> 484 us
    ppermute x0 -> x3, waiting for transfers between devices: none -> 186 us  [shards(): lax.ppermute(gradient_term, 'dp', [(dev, dev ^ hop) for dev in range(8)])]
    psum x1 -> x0, waiting for transfers between devices: 73.8 us -> none  [shards(): gradient_term = lax.psum(partial_term, 'dp')]
  transfers between devices with their start and end apart: 3 -> 5, of which waited for: 2 -> 4; matrix products, arithmetic and copies ran while one was open for 3% -> 3% of each run, Pallas kernels for 0% -> 0%
where the time goes in v1:
time: 895 us; the launch traced here: 885 us
  waiting for transfers between devices  484 us (54%)
  blocking collectives  196 us (22%)
  matrix products  98.6 us (11%)
  local copies, waits for them, and re-layouts  50.6 us (6%)
  other arithmetic  31.9 us (4%)
  between operations  14.4 us (2%)
  starting transfers between devices  10.1 us (1%)
    all_to_all x1, waiting for transfers between devices, cut_exchange(): lax.all_to_all(piece, axis, split_axis=0, concat_axis=0, tiled=True)  297 us
    all_to_all x1, blocking collectives, cut_exchange(): lax.all_to_all(piece, axis, split_axis=0, concat_axis=0, tiled=True)  196 us
    ppermute x3, waiting for transfers between devices, shards(): lax.ppermute(gradient_term, 'dp', [(dev, dev ^ hop) for dev in range(8)])  186 us
    dot_general x1, matrix products, shards(): jnp.dot(projected, arrived, preferred_element_type=jnp.float32)  47.5 us
    dot_general x5, matrix products, shards(): lax.dot_general(iterate, iterate, (((1,), (1,)), ((), ())), precision=lax...  26.7 us
    concatenate x1, other arithmetic, cut_exchange(): return laid_out(jnp.concatenate(gathered, axis=split_at), concat_dim)  22.8 us
    dot_general x5, matrix products, newton_step(): jnp.dot(inner, iterate, precision=lax.Precision.HIGHEST)  21.7 us
    scatter x1, local copies, waits for them, and re-layouts, shards(): jnp.zeros((experts * CAP, BLOCK, columns), jnp.bfloat16).at[targets]  21.4 us
  transfers between devices with their start and end apart: 5, of which 4 were waited for; matrix products, arithmetic and copies ran while one was open for 3% of the time, Pallas kernels for 0%

profile of v1, /device:TPU:0, one launch (start us, length us, event | category | flops | bytes accessed | tf_op | source)
XLA Modules:
  0.0 884.9 jit_solution(834052321272674755)
XLA Ops:
  6.5 0.9 convert_reduce_fusion
  7.4 0.7 fusion.16
  8.1 11.0 %broadcast_in_dim.7 = bf16[32,128,4096]{2,1,0:T(8,128)(2,1)} broadcast(bf16[]{:T(256)} %constant.10.clone.1), dimensions={} | broadcast | bytes 33554432 | tf_op jit(solution)/shard_map/broadcast_in_dim | solution.py:59
  19.1 21.4 %scatter_fusion = bf16[32,128,4096]{2,1,0:T(8,128)(2,1)} fusion(bf16[32,128,4096]{2,1,0:T(8,128)(2,1)} %broadcast_in_dim.7, s32[8]{0:T(128)S(1)} %fusion.16, bf16[8,128,4096]{2,1,0:T(8,128)(2,1)} %bitcast.42), kind=kCustom, calls=%fused_computation | custom fusion | bytes 25165856 | tf_op jit(solution)/shard_map/scatter | solution.py:59
  40.5 18.2 %fusion.17 = (bf16[16,1,128,4096]{3,2,1,0:T(8,128)(2,1)S(1)}, bf16[16,1,128,4096]{3,2,1,0:T(8,128)(2,1)}) fusion(bf16[16,1,256,4096]{3,2,1,0:T(8,128)(2,1)} %bitcast.40), kind=kLoop, calls=%fused_computation.32 | loop fusion | bytes 67108864 | tf_op jit(solution)/shard_map/split | solution.py:36
  58.7 195.6 %all_to_all.10 = bf16[16,1,128,4096]{3,2,1,0:T(8,128)(2,1)} all-to-all(bf16[16,1,128,4096]{3,2,1,0:T(8,128)(2,1)S(1)} %get-tuple-element.7), channel_id=1, replica_groups=mesh['dp'=8,'expert'=16] {'expert'}, dimensions={0} | all-to-all | bytes 33554432 | tf_op jit(solution)/shard_map/all_to_all | solution.py:38
  254.2 5.1 all-to-all-start.1
  259.4 0.0 all-gather.2.cloned.1.call-start
  259.4 0.7 all-gather.2.cloned.1.call-update
  260.1 296.9 %all-to-all-done.1 = bf16[16,1,128,4096]{3,2,1,0:T(8,128)(2,1)} async-done(((bf16[16,1,128,4096]{3,2,1,0:T(8,128)(2,1)}), bf16[16,1,128,4096]{3,2,1,0:T(8,128)(2,1)}, u32[]{:S(2)}, u32[]{:S(2)}) %all-to-all-start.1) | async-done | bytes 16777248 | tf_op jit(solution)/shard_map/all_to_all | solution.py:38
  557.1 22.8 %pad_maximum_fusion = bf16[16,1,256,4096]{3,2,1,0:T(8,128)(2,1)} fusion(bf16[16,1,128,4096]{3,2,1,0:T(8,128)(2,1)} %all-to-all-done.1, bf16[16,1,128,4096]{3,2,1,0:T(8,128)(2,1)} %all_to_all.10), kind=kLoop, calls=%fused_computation.1 | loop fusion | flops 67108864 | bytes 67108864 | tf_op jit(solution)/shard_map/concatenate | solution.py:39
  579.9 0.0 all-gather.2.cloned.1.call-done
  579.9 47.5 %fusion.7 = f32[256,4096]{1,0:T(8,128)} fusion(bf16[4096,4096]{1,0:T(8,128)(2,1)} %bitcast.41, bf16[1,256,4096]{2,1,0:T(8,128)(2,1)} %all-gather.2.cloned.1.call-done), kind=kOutput, calls=%fused_computation.18 | convolution fusion | flops 17180917760 | bytes 39845888 | tf_op jit(solution)/shard_map/dot_general | solution.py:67
  627.4 0.0 collective-permute-start
  627.4 7.4 collective-permute-done
  634.8 2.8 add.25
  637.5 0.0 copy-start.1
  637.5 1.6 collective-permute-start.1
  639.1 91.1 %collective-permute-done.1 = f32[256,4096]{1,0:T(8,128)S(1)} collective-permute-done((f32[256,4096]{1,0:T(8,128)S(1)}, f32[256,4096]{1,0:T(8,128)S(1)}, u32[]{:S(2)}, u32[]{:S(2)}) %collective-permute-start.1) | collective-permute-done | bytes 4194336 | tf_op jit(solution)/shard_map/ppermute | solution.py:74
  730.2 0.5 add.26
  730.7 3.3 collective-permute-start.2
  734.1 0.0 copy-done.1
  734.1 0.7 fusion.12
  734.8 1.9 fusion.10
  736.7 87.7 %collective-permute-done.2 = f32[256,4096]{1,0:T(8,128)S(1)} collective-permute-done((f32[256,4096]{1,0:T(8,128)S(1)}, f32[256,4096]{1,0:T(8,128)S(1)}, u32[]{:S(2)}, u32[]{:S(2)}) %collective-permute-start.2) | collective-permute-done | bytes 4194336 | tf_op jit(solution)/shard_map/ppermute | solution.py:74
  824.4 4.3 multiply_reduce_fusion
  829.3 0.0 copy-start
  829.3 12.2 %fusion.14 = f32[256,256]{1,0:T(8,128)S(1)} fusion(f32[256,4096]{1,0:T(8,128)} %get-tuple-element.6, f32[]{:T(128)S(6)} %sqrt.3), kind=kOutput, calls=%fused_computation.25 | convolution fusion | flops 3222274048 | bytes 4456452 | tf_op jit(solution)/shard_map/dot_general | solution.py:83
  841.5 0.0 copy-done
  841.6 4.1 multiply_subtract_fusion
  845.7 3.5 fusion.18
  849.2 4.1 fusion.3
  853.3 3.9 fusion.19
  857.3 4.1 fusion.2
  861.4 3.5 fusion.20
  864.9 4.3 fusion.1
  869.2 3.5 fusion.21
  872.8 5.1 fusion.6
Async XLA Ops:
  254.2 302.8 %all-to-all-start.1 = ((bf16[16,1,128,4096]{3,2,1,0:T(8,128)(2,1)}), bf16[16,1,128,4096]{3,2,1,0:T(8,128)(2,1)}, u32[]{:S(2)}, u32[]{:S(2)}) async-start(bf16[16,1,128,4096]{3,2,1,0:T(8,128)(2,1)} %get-tuple-element.8), calls=%async_computation.1 | async-start | bytes 33554432 | tf_op jit(solution)/shard_map/all_to_all | solution.py:38
  259.4 320.5 %all-gather.2.cloned.1.call-start = ((), (), s32[]{:S(2)}) async-start(), calls=%async_computation.2 | async-start | bytes 2359296 | tf_op jit(solution)/shard_map/all_gather | solution.py:63
  627.4 7.4 collective-permute-start
  637.5 96.5 %copy-start.1 = (bf16[1,256,4096]{2,1,0:T(8,128)(2,1)S(1)}, bf16[1,256,4096]{2,1,0:T(8,128)(2,1)}, u32[]{:S(2)}) copy-start(bf16[1,256,4096]{2,1,0:T(8,128)(2,1)} %all-gather.2.cloned.1.call-done) | copy-start | bytes 6291460
  637.5 92.7 %collective-permute-start.1 = (f32[256,4096]{1,0:T(8,128)S(1)}, f32[256,4096]{1,0:T(8,128)S(1)}, u32[]{:S(2)}, u32[]{:S(2)}) collective-permute-start(f32[256,4096]{1,0:T(8,128)S(1)} %add.25), channel_id=1, source_target_pairs={{0,32},{16,48},{32,0},{48,16},{64,96},{80,112},{96,64},{112,80},{1... | collective-permute-start | bytes 12582920 | tf_op jit(solution)/shard_map/ppermute | solution.py:74
  730.7 93.6 %collective-permute-start.2 = (f32[256,4096]{1,0:T(8,128)S(1)}, f32[256,4096]{1,0:T(8,128)S(1)}, u32[]{:S(2)}, u32[]{:S(2)}) collective-permute-start(f32[256,4096]{1,0:T(8,128)S(1)} %add.26), channel_id=1, source_target_pairs={{0,64},{16,80},{32,96},{48,112},{64,0},{80,16},{96,32},{112,48},{1... | collective-permute-start | bytes 12582920 | tf_op jit(solution)/shard_map/ppermute | solution.py:74
  829.3 12.2 %copy-start = (f32[256,4096]{1,0:T(8,128)S(1)}, f32[256,4096]{1,0:T(8,128)}, u32[]{:S(2)}) copy-start(f32[256,4096]{1,0:T(8,128)} %get-tuple-element.6) | copy-start | bytes 12582916
Sparse Core Ops, SparseCore 0:
  261.9 26.6 all-gather.1
